TPU v7x, 32 devices: a whole 2x2x4 slice. The times are simulated.
32 devices in a mesh: head: 4 (over y, core), ctx: 8 (over z, x).
Axes of the slice: x: 2, y: 2, z: 4, core: 2. Of those that a mesh axis runs over, the one named last changes fastest.
Arguments:
- queries: bfloat16 [6144, 4, 1024], P('ctx', 'head'), may hold values from -200 to 200
- keys: bfloat16 [6144, 4, 128], P('ctx', 'head'), may hold values from -6 to 6
- values: bfloat16 [6144, 4, 128], P('ctx', 'head'), may hold values from -6 to 6
- span_ids: int32 [16], replicated, may hold values from 0 to 15, as said below
Outputs:
- attn_out: bfloat16 [6144, 4, 1024], P('ctx', 'head')
Inputs may be any that keep to these rules, and one draw needn't show every extreme that they name: `span_ids`: entry 2r is below 8, entry 2r + 1 equals 15 minus entry 2r, and all entries differ.
All inputs are finite; a program needn't handle non-finite values.
Results may differ from a plain program's by a relative error of at most 0.0055.
Values may be sent and summed in bfloat16 or wider, within the bound.
A program may use at most 64 MiB of HBM per device.

v0:
```python
import jax
import jax.numpy as jnp
from jax import lax
from jax.sharding import PartitionSpec as P

masked_score = -1e30


def swapped(block, axis, stride):
    count = lax.axis_size(axis)
    route = []
    for low in range(count):
        high = low | 1 << stride
        if high != low and high < count:
            route += [(low, high), (high, low)]
    return lax.ppermute(block, axis, route)


def row_positions(row_ids, span_table, span_rows):
    blocks = row_ids // span_rows
    match = blocks[:, None] == jnp.arange(span_table.shape[0], dtype=jnp.int32)[None, :]
    return (
        jnp.sum(jnp.where(match, span_table[None, :], 0), axis=1) * span_rows + row_ids % span_rows
    )


def update(state, query_part, query_pos, key_block, value_block, key_pos, score_scale):
    numerator, run_max, weight_sum = state
    scores = (
        jnp.einsum("qgd,kd->qgk", query_part, key_block, preferred_element_type=jnp.float32)
        * score_scale
    )
    allowed = key_pos[None, None, :] <= query_pos[:, None, None]
    scores = jnp.where(allowed, scores, masked_score)
    new_max = jnp.maximum(run_max, jnp.max(scores, axis=2))
    factor = jnp.exp(run_max - new_max)
    weights = jnp.where(allowed, jnp.exp(scores - new_max[:, :, None]), 0.0)
    weight_sum = weight_sum * factor + jnp.sum(weights, axis=2)
    mixed = jnp.einsum(
        "qgk,kd->qgd", weights.astype(jnp.bfloat16), value_block, preferred_element_type=jnp.float32
    )
    return (numerator * factor[:, :, None] + mixed, new_max, weight_sum)


def local(queries, keys, values, span_ids):
    tok_rows = queries.shape[0]
    span_rows = tok_rows // 2
    head_dim = keys.shape[2]
    group_size = queries.shape[2] // head_dim
    score_scale = head_dim ** (-0.5)
    my_rank = lax.axis_index("ctx")
    query_heads = queries.reshape(tok_rows, group_size, head_dim)
    key_rows = keys.reshape(tok_rows, head_dim)
    value_rows = values.reshape(tok_rows, head_dim)
    local_ids = jnp.arange(tok_rows, dtype=jnp.int32)
    query_pos = row_positions(my_rank * tok_rows + local_ids, span_ids, span_rows)
    halves = [
        (
            query_heads[half_no * span_rows : (half_no + 1) * span_rows],
            query_pos[half_no * span_rows : (half_no + 1) * span_rows],
        )
        for half_no in range(2)
    ]

    def absorb(state, key_buf, value_buf, row_ids):
        count = key_buf.shape[0]
        pieces = count // span_rows

        def step(carry, inputs_now):
            key_block, value_block, block_ids = inputs_now
            key_pos = row_positions(block_ids, span_ids, span_rows)
            result = []
            for half_no in range(2):
                query_part, part_pos = halves[half_no]

                def attend(state_now, part_now=query_part, pos_now=part_pos):
                    return update(
                        state_now, part_now, pos_now, key_block, value_block, key_pos, score_scale
                    )

                result.append(
                    lax.cond(
                        jnp.min(key_pos) <= jnp.max(part_pos),
                        attend,
                        lambda state_now: state_now,
                        carry[half_no],
                    )
                )
            return (tuple(result), None)

        state, unused = lax.scan(
            step,
            state,
            (
                key_buf.reshape(pieces, span_rows, head_dim),
                value_buf.reshape(pieces, span_rows, head_dim),
                row_ids.reshape(pieces, span_rows),
            ),
        )
        return state

    empty_half = (
        jnp.zeros((span_rows, group_size, head_dim), jnp.float32),
        jnp.full((span_rows, group_size), masked_score, jnp.float32),
        jnp.zeros((span_rows, group_size), jnp.float32),
    )
    start_state = (empty_half, empty_half)
    final = absorb(start_state, key_rows, value_rows, my_rank * tok_rows + local_ids)
    key_buf, value_buf = (key_rows, value_rows)
    owners = jnp.reshape(my_rank, (1,))
    for bit_no in range(lax.axis_size("ctx").bit_length() - 1):
        got_keys, got_values = swapped((key_buf, value_buf), "ctx", bit_no)
        partner = jnp.bitwise_xor(owners, 1 << bit_no)
        row_ids = (partner[:, None] * tok_rows + local_ids[None, :]).reshape(-1)
        final = absorb(final, got_keys, got_values, row_ids)
        key_buf = jnp.concatenate((key_buf, got_keys), axis=0)
        value_buf = jnp.concatenate((value_buf, got_values), axis=0)
        owners = jnp.concatenate((owners, partner), axis=0)
    outputs = [(state[0] / state[2][:, :, None]).astype(jnp.bfloat16) for state in final]
    return jnp.concatenate(outputs, axis=0).reshape(tok_rows, 1, group_size * head_dim)


def solution(mesh):
    in_specs = (P("ctx", "head", None), P("ctx", "head", None), P("ctx", "head", None), P())
    out_specs = P("ctx", "head", None)
    return jax.shard_map(local, mesh=mesh, in_specs=in_specs, out_specs=out_specs, check_vma=False)
```

profile of v0, /device:TPU:0, one launch (start us, length us, event | category | flops | bytes accessed | tf_op | source)
XLA Modules:
  0.0 213.0 jit_solution(3576558799570766612)
XLA Ops:
  0.0 3.0 %collective-permute-start = (bf16[768,128]{1,0:T(8,128)(2,1)}, bf16[768,128]{1,0:T(8,128)(2,1)}, u32[]{:S(2)}, u32[]{:S(2)}) collective-permute-start(bf16[768,128]{1,0:T(8,128)(2,1)} %bitcast.110), channel_id=1, source_target_pairs={{0,1},{1,0},{2,3},{3,2},{4,5},{5,4},{6,7},{7,6},{8,9},{9,8},{10,11... | collective-permute-start | bytes 589832 | tf_op jit(solution)/shard_map/ppermute | solution.py:16
  8.9 24.2 %while.88 = (s32[]{:T(128)}, f32[384,8,128]{2,0,1:T(8,128)S(1)}, f32[384,8]{0,1:T(8,128)S(1)}, f32[384,8]{0,1:T(8,128)S(1)}, f32[384,8,128]{2,0,1:T(8,128)}, /*i...) while((s32[]{:T(128)}, f32[384,8,128]{2,0,1:T(8,128)S(1)}, ...), condition=%wide.region_14.15_spmd, body=%wide.region_3.0_spmd.sunk | while | flops 1240534656 | bytes 51930480 | solution.py:91
  12.4 5.3 %conditional.17 = ((f32[384,8,128]{2,0,1:T(8,128)}, f32[384,8]{0,1:T(8,128)S(1)}, f32[384,8]{0,1:T(8,128)S(1)})) conditional(s32[]{:T(128)} %convert_element_type.123, (f32[384,8,128]{2,0,1:T(8,128)}, f32[384,8]{0,1:T(8,128)S(1)}, f32[384,8]{0,1:T(8,128)S(1)}) %tuple.217, (s32[384]{0:T(512)S(1)}, s32[384]{0:T(512)S(1)}, ...), branch_computations={%region_10.10_spmd, %region_11.13_spmd} | conditional | flops 620255232 | bytes 32050292 | solution.py:82
  18.9 4.2 %conditional.16 = ((f32[384,8,128]{2,0,1:T(8,128)S(1)}, f32[384,8]{0,1:T(8,128)S(1)}, f32[384,8]{0,1:T(8,128)S(1)})) conditional(s32[]{:T(128)} %convert_element_type.122, (f32[384,8,128]{2,0,1:T(8,128)S(1)}, f32[384,8]{0,1:T(8,128)S(1)}, f32[384,8]{0,1:T(8,128)S(1)}) %tuple.215, (s32[384]{0:T(512)S(1)}, s32[384]{0:T(512)S(1)}, ...), branch_computations={%region_6.6_spmd, %region_7.9_spmd} | conditional | flops 620255232 | bytes 19467324 | solution.py:82
  26.6 5.3 %conditional.17 = ((f32[384,8,128]{2,0,1:T(8,128)}, f32[384,8]{0,1:T(8,128)S(1)}, f32[384,8]{0,1:T(8,128)S(1)})) conditional(s32[]{:T(128)} %convert_element_type.123, (f32[384,8,128]{2,0,1:T(8,128)}, f32[384,8]{0,1:T(8,128)S(1)}, f32[384,8]{0,1:T(8,128)S(1)}) %tuple.217, (s32[384]{0:T(512)S(1)}, s32[384]{0:T(512)S(1)}, ...), branch_computations={%region_10.10_spmd, %region_11.13_spmd} | conditional | flops 620255232 | bytes 32050292 | solution.py:82
  35.5 2.1 collective-permute-start.2
  39.4 20.5 %while.89 = (s32[]{:T(128)}, f32[384,8,128]{2,0,1:T(8,128)S(1)}, f32[384,8]{0,1:T(8,128)S(1)}, f32[384,8]{0,1:T(8,128)S(1)}, f32[384,8,128]{2,0,1:T(8,128)}, /*i...) while((s32[]{:T(128)}, f32[384,8,128]{2,0,1:T(8,128)S(1)}, ...), condition=%wide.region_26.27_spmd, body=%wide.region_15.26_spmd.sunk | while | flops 1240534656 | bytes 51930480 | solution.py:91
  43.1 5.3 %conditional.19 = ((f32[384,8,128]{2,0,1:T(8,128)}, f32[384,8]{0,1:T(8,128)S(1)}, f32[384,8]{0,1:T(8,128)S(1)})) conditional(s32[]{:T(128)} %convert_element_type.125, (f32[384,8,128]{2,0,1:T(8,128)}, f32[384,8]{0,1:T(8,128)S(1)}, f32[384,8]{0,1:T(8,128)S(1)}) %tuple.225, (s32[384]{0:T(512)S(1)}, s32[384]{0:T(512)S(1)}, ...), branch_computations={%region_22.22_spmd, %region_23.25_spmd} | conditional | flops 620255232 | bytes 32050292 | solution.py:82
  45.3 1.9 multiply_add_fusion.6
  53.3 5.3 %conditional.19 = ((f32[384,8,128]{2,0,1:T(8,128)}, f32[384,8]{0,1:T(8,128)S(1)}, f32[384,8]{0,1:T(8,128)S(1)})) conditional(s32[]{:T(128)} %convert_element_type.125, (f32[384,8,128]{2,0,1:T(8,128)}, f32[384,8]{0,1:T(8,128)S(1)}, f32[384,8]{0,1:T(8,128)S(1)}) %tuple.225, (s32[384]{0:T(512)S(1)}, s32[384]{0:T(512)S(1)}, ...), branch_computations={%region_22.22_spmd, %region_23.25_spmd} | conditional | flops 620255232 | bytes 32050292 | solution.py:82
  59.9 2.0 pad_maximum_fusion.1
  61.9 3.0 %collective-permute-start.4 = (bf16[3072,128]{1,0:T(8,128)(2,1)}, bf16[3072,128]{1,0:T(8,128)(2,1)}, u32[]{:S(2)}, u32[]{:S(2)}) collective-permute-start(bf16[3072,128]{1,0:T(8,128)(2,1)} %pad_maximum_fusion.1), channel_id=1, source_target_pairs={{0,4},{4,0},{1,5},{5,1},{2,6},{6,2},{3,7},{7,3},{8,12},{12,8},{9,1... | collective-permute-start | bytes 2359304 | tf_op jit(solution)/shard_map/ppermute | solution.py:16
  64.9 2.1 pad_maximum_fusion.2
  67.0 37.8 %while.90 = (s32[]{:T(128)}, f32[384,8,128]{2,0,1:T(8,128)S(1)}, f32[384,8]{0,1:T(8,128)S(1)}, f32[384,8]{0,1:T(8,128)S(1)}, f32[384,8,128]{2,0,1:T(8,128)}, /*i...) while((s32[]{:T(128)}, f32[384,8,128]{2,0,1:T(8,128)S(1)}, ...), condition=%wide.region_38.39_spmd, body=%wide.region_27.38_spmd.sunk | while | flops 1240534656 | bytes 51143992 | solution.py:91
  70.0 5.3 %conditional.21 = ((f32[384,8,128]{2,0,1:T(8,128)}, f32[384,8]{0,1:T(8,128)S(1)}, f32[384,8]{0,1:T(8,128)S(1)})) conditional(s32[]{:T(128)} %convert_element_type.127, (f32[384,8,128]{2,0,1:T(8,128)}, f32[384,8]{0,1:T(8,128)S(1)}, f32[384,8]{0,1:T(8,128)S(1)}) %tuple.233, (s32[384]{0:T(512)S(1)}, s32[384]{0:T(512)S(1)}, ...), branch_computations={%region_34.34_spmd, %region_35.37_spmd} | conditional | flops 620255232 | bytes 31657048 | solution.py:82
  72.2 1.9 multiply_add_fusion.10
  79.4 5.3 %conditional.21 = ((f32[384,8,128]{2,0,1:T(8,128)}, f32[384,8]{0,1:T(8,128)S(1)}, f32[384,8]{0,1:T(8,128)S(1)})) conditional(s32[]{:T(128)} %convert_element_type.127, (f32[384,8,128]{2,0,1:T(8,128)}, f32[384,8]{0,1:T(8,128)S(1)}, f32[384,8]{0,1:T(8,128)S(1)}) %tuple.233, (s32[384]{0:T(512)S(1)}, s32[384]{0:T(512)S(1)}, ...), branch_computations={%region_34.34_spmd, %region_35.37_spmd} | conditional | flops 620255232 | bytes 31657048 | solution.py:82
  88.9 5.3 %conditional.21 = ((f32[384,8,128]{2,0,1:T(8,128)}, f32[384,8]{0,1:T(8,128)S(1)}, f32[384,8]{0,1:T(8,128)S(1)})) conditional(s32[]{:T(128)} %convert_element_type.127, (f32[384,8,128]{2,0,1:T(8,128)}, f32[384,8]{0,1:T(8,128)S(1)}, f32[384,8]{0,1:T(8,128)S(1)}) %tuple.233, (s32[384]{0:T(512)S(1)}, s32[384]{0:T(512)S(1)}, ...), branch_computations={%region_34.34_spmd, %region_35.37_spmd} | conditional | flops 620255232 | bytes 31657048 | solution.py:82
  98.3 5.3 %conditional.21 = ((f32[384,8,128]{2,0,1:T(8,128)}, f32[384,8]{0,1:T(8,128)S(1)}, f32[384,8]{0,1:T(8,128)S(1)})) conditional(s32[]{:T(128)} %convert_element_type.127, (f32[384,8,128]{2,0,1:T(8,128)}, f32[384,8]{0,1:T(8,128)S(1)}, f32[384,8]{0,1:T(8,128)S(1)}) %tuple.233, (s32[384]{0:T(512)S(1)}, s32[384]{0:T(512)S(1)}, ...), branch_computations={%region_34.34_spmd, %region_35.37_spmd} | conditional | flops 620255232 | bytes 31657048 | solution.py:82
  104.8 11.7 %collective-permute-done.4 = bf16[3072,128]{1,0:T(8,128)(2,1)} collective-permute-done((bf16[3072,128]{1,0:T(8,128)(2,1)}, bf16[3072,128]{1,0:T(8,128)(2,1)}, u32[]{:S(2)}, u32[]{:S(2)}) %collective-permute-start.4) | collective-permute-done | bytes 786464 | tf_op jit(solution)/shard_map/ppermute | solution.py:16
  116.5 15.7 %collective-permute-done.5 = bf16[3072,128]{1,0:T(8,128)(2,1)} collective-permute-done((bf16[3072,128]{1,0:T(8,128)(2,1)}, bf16[3072,128]{1,0:T(8,128)(2,1)}, u32[]{:S(2)}, u32[]{:S(2)}) %collective-permute-start.5) | collective-permute-done | bytes 786464 | tf_op jit(solution)/shard_map/ppermute | solution.py:16
  132.2 75.5 %while.91 = (s32[]{:T(128)}, f32[384,8,128]{2,0,1:T(8,128)S(1)}, f32[384,8]{0,1:T(8,128)S(1)}, f32[384,8]{0,1:T(8,128)S(1)}, f32[384,8,128]{2,0,1:T(8,128)}, /*i...) while((s32[]{:T(128)}, f32[384,8,128]{2,0,1:T(8,128)S(1)}, ...), condition=%wide.region_50.51_spmd, body=%wide.region_39.50_spmd.sunk | while | flops 1240534656 | bytes 51143992 | solution.py:91
  135.2 5.3 %conditional.23 = ((f32[384,8,128]{2,0,1:T(8,128)}, f32[384,8]{0,1:T(8,128)S(1)}, f32[384,8]{0,1:T(8,128)S(1)})) conditional(s32[]{:T(128)} %convert_element_type.129, (f32[384,8,128]{2,0,1:T(8,128)}, f32[384,8]{0,1:T(8,128)S(1)}, f32[384,8]{0,1:T(8,128)S(1)}) %tuple.241, (s32[384]{0:T(512)S(1)}, s32[384]{0:T(512)S(1)}, ...), branch_computations={%region_46.46_spmd, %region_47.49_spmd} | conditional | flops 620255232 | bytes 31657048 | solution.py:82
  141.7 4.1 %conditional.22 = ((f32[384,8,128]{2,0,1:T(8,128)S(1)}, f32[384,8]{0,1:T(8,128)S(1)}, f32[384,8]{0,1:T(8,128)S(1)})) conditional(s32[]{:T(128)} %convert_element_type.128, (f32[384,8,128]{2,0,1:T(8,128)S(1)}, f32[384,8]{0,1:T(8,128)S(1)}, f32[384,8]{0,1:T(8,128)S(1)}) %tuple.239, (s32[384]{0:T(512)S(1)}, s32[384]{0:T(512)S(1)}, ...), branch_computations={%region_42.42_spmd, %region_43.45_spmd} | conditional | flops 620255232 | bytes 19074080 | solution.py:82
  153.2 5.3 %conditional.23 = ((f32[384,8,128]{2,0,1:T(8,128)}, f32[384,8]{0,1:T(8,128)S(1)}, f32[384,8]{0,1:T(8,128)S(1)})) conditional(s32[]{:T(128)} %convert_element_type.129, (f32[384,8,128]{2,0,1:T(8,128)}, f32[384,8]{0,1:T(8,128)S(1)}, f32[384,8]{0,1:T(8,128)S(1)}) %tuple.241, (s32[384]{0:T(512)S(1)}, s32[384]{0:T(512)S(1)}, ...), branch_computations={%region_46.46_spmd, %region_47.49_spmd} | conditional | flops 620255232 | bytes 31657048 | solution.py:82
  162.8 5.3 %conditional.23 = ((f32[384,8,128]{2,0,1:T(8,128)}, f32[384,8]{0,1:T(8,128)S(1)}, f32[384,8]{0,1:T(8,128)S(1)})) conditional(s32[]{:T(128)} %convert_element_type.129, (f32[384,8,128]{2,0,1:T(8,128)}, f32[384,8]{0,1:T(8,128)S(1)}, f32[384,8]{0,1:T(8,128)S(1)}) %tuple.241, (s32[384]{0:T(512)S(1)}, s32[384]{0:T(512)S(1)}, ...), branch_computations={%region_46.46_spmd, %region_47.49_spmd} | conditional | flops 620255232 | bytes 31657048 | solution.py:82
  172.4 5.3 %conditional.23 = ((f32[384,8,128]{2,0,1:T(8,128)}, f32[384,8]{0,1:T(8,128)S(1)}, f32[384,8]{0,1:T(8,128)S(1)})) conditional(s32[]{:T(128)} %convert_element_type.129, (f32[384,8,128]{2,0,1:T(8,128)}, f32[384,8]{0,1:T(8,128)S(1)}, f32[384,8]{0,1:T(8,128)S(1)}) %tuple.241, (s32[384]{0:T(512)S(1)}, s32[384]{0:T(512)S(1)}, ...), branch_computations={%region_46.46_spmd, %region_47.49_spmd} | conditional | flops 620255232 | bytes 31657048 | solution.py:82
  182.0 5.3 %conditional.23 = ((f32[384,8,128]{2,0,1:T(8,128)}, f32[384,8]{0,1:T(8,128)S(1)}, f32[384,8]{0,1:T(8,128)S(1)})) conditional(s32[]{:T(128)} %convert_element_type.129, (f32[384,8,128]{2,0,1:T(8,128)}, f32[384,8]{0,1:T(8,128)S(1)}, f32[384,8]{0,1:T(8,128)S(1)}) %tuple.241, (s32[384]{0:T(512)S(1)}, s32[384]{0:T(512)S(1)}, ...), branch_computations={%region_46.46_spmd, %region_47.49_spmd} | conditional | flops 620255232 | bytes 31657048 | solution.py:82
  191.6 5.3 %conditional.23 = ((f32[384,8,128]{2,0,1:T(8,128)}, f32[384,8]{0,1:T(8,128)S(1)}, f32[384,8]{0,1:T(8,128)S(1)})) conditional(s32[]{:T(128)} %convert_element_type.129, (f32[384,8,128]{2,0,1:T(8,128)}, f32[384,8]{0,1:T(8,128)S(1)}, f32[384,8]{0,1:T(8,128)S(1)}) %tuple.241, (s32[384]{0:T(512)S(1)}, s32[384]{0:T(512)S(1)}, ...), branch_computations={%region_46.46_spmd, %region_47.49_spmd} | conditional | flops 620255232 | bytes 31657048 | solution.py:82
  201.1 5.3 %conditional.23 = ((f32[384,8,128]{2,0,1:T(8,128)}, f32[384,8]{0,1:T(8,128)S(1)}, f32[384,8]{0,1:T(8,128)S(1)})) conditional(s32[]{:T(128)} %convert_element_type.129, (f32[384,8,128]{2,0,1:T(8,128)}, f32[384,8]{0,1:T(8,128)S(1)}, f32[384,8]{0,1:T(8,128)S(1)}) %tuple.241, (s32[384]{0:T(512)S(1)}, s32[384]{0:T(512)S(1)}, ...), branch_computations={%region_46.46_spmd, %region_47.49_spmd} | conditional | flops 620255232 | bytes 31657048 | solution.py:82
  207.7 2.1 %divide_convert_fusion = (bf16[384,8,128]{2,0,1:T(8,128)(2,1)S(1)}, bf16[384,8,128]{2,0,1:T(8,128)(2,1)S(1)}) fusion(f32[384,8,128]{2,0,1:T(8,128)} %get-tuple-element.1155, f32[384,8]{0,1:T(8,128)S(1)} %get-tuple-element.1156, f32[384,8,128]{2,0,1:T(8,128)S(1)} %get-tuple-element.1153, f32[384,8]{0,1:T(8,128)S(1)} %get-tuple-element.1154), kind=kLoop, calls=%fused_computation.185 | loop fusion | flops 1572864 | bytes 4743168 | tf_op jit(solution)/shard_map/convert_element_type | solution.py:119
  211.0 2.1 reshape.493
  (343 shorter events, 124.5 us)
Async XLA Ops:
  0.0 33.8 %collective-permute-start = (bf16[768,128]{1,0:T(8,128)(2,1)}, bf16[768,128]{1,0:T(8,128)(2,1)}, u32[]{:S(2)}, u32[]{:S(2)}) collective-permute-start(bf16[768,128]{1,0:T(8,128)(2,1)} %bitcast.110), channel_id=1, source_target_pairs={{0,1},{1,0},{2,3},{3,2},{4,5},{5,4},{6,7},{7,6},{8,9},{9,8},{10,11... | collective-permute-start | bytes 589832 | tf_op jit(solution)/shard_map/ppermute | solution.py:16
  3.0 34.6 %collective-permute-start.1 = (bf16[768,128]{1,0:T(8,128)(2,1)}, bf16[768,128]{1,0:T(8,128)(2,1)}, u32[]{:S(2)}, u32[]{:S(2)}) collective-permute-start(bf16[768,128]{1,0:T(8,128)(2,1)} %bitcast.114), channel_id=1, source_target_pairs={{0,1},{1,0},{2,3},{3,2},{4,5},{5,4},{6,7},{7,6},{8,9},{9,8},{10,11... | collective-permute-start | bytes 589832 | tf_op jit(solution)/shard_map/ppermute | solution.py:16
  6.0 2.9 %copy-start.8 = (bf16[768,1,128]{2,0,1:T(8,128)(2,1)S(1)}, bf16[768,1,128]{2,0,1:T(8,128)(2,1)}, u32[]{:S(2)}) copy-start(bf16[768,1,128]{2,0,1:T(8,128)(2,1)} %param.29) | copy-start | bytes 589828
  6.0 2.9 %copy-start.13 = (s32[16]{0:T(128)S(1)}, s32[16]{0:T(128)}, u32[]{:S(2)}) copy-start(s32[16]{0:T(128)} %param.31) | copy-start | bytes 196
  12.6 2.1 copy-start
  12.6 2.1 copy-start.9
  16.6 1.1 copy-start.1
  19.1 2.1 copy-start.10
  26.8 2.1 copy-start
  26.8 2.1 copy-start.9
  30.8 1.1 copy-start.1
  35.5 24.4 %collective-permute-start.2 = (bf16[1536,128]{1,0:T(8,128)(2,1)}, bf16[1536,128]{1,0:T(8,128)(2,1)}, u32[]{:S(2)}, u32[]{:S(2)}) collective-permute-start(bf16[1536,128]{1,0:T(8,128)(2,1)} %pad_maximum_fusion.3), channel_id=1, source_target_pairs={{0,2},{2,0},{1,3},{3,1},{4,6},{6,4},{5,7},{7,5},{8,10},{10,8},{9,1... | collective-permute-start | bytes 1179656 | tf_op jit(solution)/shard_map/ppermute | solution.py:16
  39.4 25.5 %collective-permute-start.3 = (bf16[1536,128]{1,0:T(8,128)(2,1)}, bf16[1536,128]{1,0:T(8,128)(2,1)}, u32[]{:S(2)}, u32[]{:S(2)}) collective-permute-start(bf16[1536,128]{1,0:T(8,128)(2,1)} %pad_maximum_fusion.4), channel_id=1, source_target_pairs={{0,2},{2,0},{1,3},{3,1},{4,6},{6,4},{5,7},{7,5},{8,10},{10,8},{9,1... | collective-permute-start | bytes 1179656 | tf_op jit(solution)/shard_map/ppermute | solution.py:16
  43.2 2.1 copy-start.2
  43.2 2.1 copy-start.11
  53.5 2.1 copy-start.2
  53.5 2.1 copy-start.11
  61.9 54.6 %collective-permute-start.4 = (bf16[3072,128]{1,0:T(8,128)(2,1)}, bf16[3072,128]{1,0:T(8,128)(2,1)}, u32[]{:S(2)}, u32[]{:S(2)}) collective-permute-start(bf16[3072,128]{1,0:T(8,128)(2,1)} %pad_maximum_fusion.1), channel_id=1, source_target_pairs={{0,4},{4,0},{1,5},{5,1},{2,6},{6,2},{3,7},{7,3},{8,12},{12,8},{9,1... | collective-permute-start | bytes 2359304 | tf_op jit(solution)/shard_map/ppermute | solution.py:16
  67.0 65.2 %collective-permute-start.5 = (bf16[3072,128]{1,0:T(8,128)(2,1)}, bf16[3072,128]{1,0:T(8,128)(2,1)}, u32[]{:S(2)}, u32[]{:S(2)}) collective-permute-start(bf16[3072,128]{1,0:T(8,128)(2,1)} %pad_maximum_fusion.2), channel_id=1, source_target_pairs={{0,4},{4,0},{1,5},{5,1},{2,6},{6,2},{3,7},{7,3},{8,12},{12,8},{9,1... | collective-permute-start | bytes 2359304 | tf_op jit(solution)/shard_map/ppermute | solution.py:16
  70.1 2.1 copy-start.4
  79.6 2.1 copy-start.4
  89.0 2.1 copy-start.4
  93.0 1.1 copy-start.5
  98.5 2.1 copy-start.4
  102.5 1.1 copy-start.5
  135.4 2.1 copy-start.6
  153.4 2.1 copy-start.6
  163.0 2.1 copy-start.6
  172.6 2.1 copy-start.6
  182.1 2.1 copy-start.6
  191.7 2.1 copy-start.6
  201.3 2.1 copy-start.6
  (11 other events, 12.6 us)
where the time goes:
time: 214 us; the launch traced here: 213 us
  matrix products  47 us (22%)
  other arithmetic  46.7 us (22%)
  local copies, waits for them, and re-layouts  42.7 us (20%)
  loops' own time  41.1 us (19%)
  waiting for transfers between devices  27.4 us (13%)
  starting transfers between devices  8.12 us (4%)
    another operation x4, loops' own time, absorb(): lax.scan(step, state, (key_buf.reshape(pieces, span_rows, head_dim), valu...  39.4 us
    dot_general x17, matrix products, update(): jnp.einsum('qgk,kd->qgd', weights.astype(jnp.bfloat16), value_block, pref...  32 us
    ppermute x6, waiting for transfers between devices, swapped(): return lax.ppermute(block, axis, route)  27.4 us
    reduce_sum x17, other arithmetic, update(): weight_sum = weight_sum * factor + jnp.sum(weights, axis=2)  19.3 us
    squeeze x16, local copies, waits for them, and re-layouts, absorb(): lax.scan(step, state, (key_buf.reshape(pieces, span_rows, head_dim), valu...  17.7 us
    cond x87, local copies, waits for them, and re-layouts  17.2 us
    dot_general x17, matrix products, update(): jnp.einsum('qgd,kd->qgk', query_part, key_block, preferred_element_type=j...  15 us
    reduce_min x16, other arithmetic, step(): jnp.min(key_pos) <= jnp.max(part_pos)  10.5 us
  transfers between devices with their start and end apart: 6, of which 2 were waited for; matrix products, arithmetic and copies ran while one was open for 31% of the time, Pallas kernels for 0%

commit v1 on v0

v1 whole, which is shorter than its diff:
```python
import functools
import math

import jax
import jax.numpy as jnp
from jax import lax
from jax.experimental import pallas as pl
from jax.experimental.pallas import tpu as pltpu
from jax.sharding import PartitionSpec as P

MESH = pl.DeviceIdType.MESH
LOW, HIGH = 0, 1
TO_PARTNER, TO_NEXT, TO_PREV = 0, 1, 2
MASKED = -1e30
HEADS_PER_STEP = 2


def kernel(
    count, head_dim, ids, q_hbm, k_hbm, v_hbm, o_hbm,
    q, kv, kv_pick, acc, top, total, out, in_sem, out_sem, send_sem, recv_sem,
):
    groups, rows, _ = q.shape
    span = rows // 2
    line = count // 2
    lanes = head_dim
    pieces = span // lanes
    scale = head_dim ** (-0.5) * math.log2(math.e)
    me = lax.axis_index("ctx")
    z = me // 2
    x = me % 2
    partner = z * 2 + 1 - x

    def kv_in(half, which, src):
        return pltpu.make_async_copy(
            src.at[pl.ds(half * span, span), :], kv.at[me, half, which], in_sem.at[half, which]
        )

    def q_in(group):
        return pltpu.make_async_copy(
            q_hbm.at[:, pl.ds(group * lanes, lanes)], q.at[group], in_sem.at[2 + group, 0]
        )

    for half in range(2):
        kv_in(half, 0, k_hbm).start()
        kv_in(half, 1, v_hbm).start()
    for group in range(groups):
        q_in(group).start()

    barrier = pltpu.get_barrier_semaphore()
    pl.semaphore_signal(barrier, inc=1, device_id={"ctx": partner}, device_id_type=MESH)

    @pl.when(z > 0)
    def _():
        pl.semaphore_signal(barrier, inc=1, device_id={"ctx": me - 2}, device_id_type=MESH)

    @pl.when(z < line - 1)
    def _():
        pl.semaphore_signal(barrier, inc=1, device_id={"ctx": me + 2}, device_id_type=MESH)

    near = 1 + jnp.where(z > 0, 1, 0) + jnp.where(z < line - 1, 1, 0)
    pl.semaphore_wait(barrier, near)

    def sent(owner, half, way):
        target = (partner, me + 2, me - 2)[way]
        return pltpu.make_async_remote_copy(
            src_ref=kv.at[owner, half],
            dst_ref=kv.at[owner, half],
            send_sem=send_sem.at[owner, half, way],
            recv_sem=recv_sem.at[owner, half],
            device_id={"ctx": target},
            device_id_type=MESH,
        )

    for half in range(2):
        kv_in(half, 0, k_hbm).wait()
        kv_in(half, 1, v_hbm).wait()

        @pl.when(z < line - 1)
        def _():
            sent(me, half, TO_NEXT).start()

        @pl.when(z > 0)
        def _():
            sent(me, half, TO_PREV).start()

        sent(me, half, TO_PARTNER).start()

    def relay(step, half):
        before = z - step
        after = z + step

        @pl.when(before >= 0)
        def _():
            owner = before * 2 + x
            sent(owner, half, TO_PARTNER).wait_recv()

            @pl.when(z < line - 1)
            def _():
                sent(owner, half, TO_NEXT).start()

            sent(owner, half, TO_PARTNER).start()

        @pl.when(after < line)
        def _():
            owner = after * 2 + x
            sent(owner, half, TO_PARTNER).wait_recv()

            @pl.when(z > 0)
            def _():
                sent(owner, half, TO_PREV).start()

            sent(owner, half, TO_PARTNER).start()

    for group in range(groups):
        q_in(group).wait()

    def score(q_part, k_part):
        return lax.dot_general(
            q_part, k_part, (((1,), (1,)), ((), ())), preferred_element_type=jnp.float32
        )

    def row_top(s):
        best = s[:, :lanes]
        for piece in range(1, pieces):
            best = jnp.maximum(best, s[:, piece * lanes : (piece + 1) * lanes])
        return jnp.max(best, axis=1, keepdims=True)

    def weigh(s, m):
        parts = [
            jnp.exp2((s[:, piece * lanes : (piece + 1) * lanes] - m) * scale)
            for piece in range(pieces)
        ]
        summed = parts[0]
        for part in parts[1:]:
            summed = summed + part
        return jnp.concatenate([part.astype(jnp.bfloat16) for part in parts], axis=1), summed

    def mix(p, v_part):
        return jnp.dot(p, v_part, preferred_element_type=jnp.float32)

    def over_groups(body):
        def step(index, carry):
            for inner in range(HEADS_PER_STEP):
                body(index * HEADS_PER_STEP + inner)
            return carry

        lax.fori_loop(0, groups // HEADS_PER_STEP, step, 0)

    def half_q(group, half):
        return q[group, half * span : (half + 1) * span, :]

    def own_span(half):
        row_no = lax.broadcasted_iota(jnp.int32, (span, span), 0)
        key_no = lax.broadcasted_iota(jnp.int32, (span, span), 1)

        def body(group):
            s = score(half_q(group, half), kv[me, half, 0])
            s = jnp.where(key_no <= row_no, s, MASKED)
            m = jnp.broadcast_to(row_top(s), (span, lanes))
            p, summed = weigh(s, m)
            top[half, group] = m
            total[half, group] = summed
            acc[half, group] = mix(p, kv[me, half, 1])

        over_groups(body)

    def high_on_low(owner):
        def body(group):
            s = score(half_q(group, HIGH), kv[owner, LOW, 0])
            old = top[HIGH, group]
            m = jnp.maximum(old, row_top(s))
            fade = jnp.exp2((old - m) * scale)
            p, summed = weigh(s, m)
            top[HIGH, group] = m
            total[HIGH, group] = total[HIGH, group] * fade + summed
            acc[HIGH, group] = acc[HIGH, group] * fade + mix(p, kv[owner, LOW, 1])

        over_groups(body)

    def same_half(owner):
        flag = jnp.where(ids[2 * owner] > ids[2 * me], 1, 0)
        is_high = jnp.full((span, lanes), flag, jnp.int32) == 1
        for which in range(2):
            kv_pick[which] = jnp.where(is_high, kv[owner, HIGH, which], kv[owner, LOW, which])

        def body(group):
            s = score(jnp.where(is_high, half_q(group, HIGH), half_q(group, LOW)), kv_pick[0])
            tops = [top[half, group] for half in range(2)]
            old = jnp.where(is_high, tops[HIGH], tops[LOW])
            m = jnp.maximum(old, row_top(s))
            fade = jnp.exp2((old - m) * scale)
            p, summed = weigh(s, m)
            top[LOW, group] = jnp.where(is_high, tops[LOW], m)
            top[HIGH, group] = jnp.where(is_high, m, tops[HIGH])
            added = mix(p, kv_pick[1])
            for ref, extra in ((total, summed), (acc, added)):
                low_now, high_now = ref[LOW, group], ref[HIGH, group]
                new = jnp.where(is_high, high_now, low_now) * fade + extra
                ref[LOW, group] = jnp.where(is_high, low_now, new)
                ref[HIGH, group] = jnp.where(is_high, new, high_now)

        over_groups(body)

    own_span(LOW)
    own_span(HIGH)
    high_on_low(me)

    short = jnp.minimum(z, line - 1 - z)
    far_side = jnp.where(z <= line - 1 - z, 1, -1)

    def line_place(order):
        paired = jnp.where(order % 2 == 1, -1, 1) * ((order + 1) // 2)
        alone = far_side * (order - short)
        return z + jnp.where(order <= 2 * short, paired, alone)

    def visit(index, carry):
        on_line = index % 2
        step = index // 2 + 1
        order = index // 2 + on_line
        owner = line_place(order) * 2 + jnp.where(on_line == 1, x, 1 - x)
        moving = jnp.logical_and(on_line == 0, step < line)
        for half in range(2):

            @pl.when(moving)
            def _():
                relay(step, half)

            @pl.when(on_line == 0)
            def _():
                sent(owner, half, TO_PARTNER).wait_recv()

            if half == LOW:
                high_on_low(owner)
            else:
                same_half(owner)
        return carry

    lax.fori_loop(0, count - 1, visit, 0)

    def finish(group):
        for half in range(2):
            weight = jnp.sum(total[half, group], axis=1, keepdims=True)
            out[group, half * span : (half + 1) * span, :] = (
                acc[half, group] / weight
            ).astype(out.dtype)

    def result(group):
        return pltpu.make_async_copy(
            out.at[group], o_hbm.at[:, pl.ds(group * lanes, lanes)], out_sem.at[group]
        )

    for group in range(groups):
        finish(group)
        result(group).start()

    def settle(place, carry):
        owner = place * 2 + x
        for half in range(2):
            sent(owner, half, TO_PARTNER).wait_send()

            @pl.when(jnp.logical_and(place <= z, z < line - 1))
            def _():
                sent(owner, half, TO_NEXT).wait_send()

            @pl.when(jnp.logical_and(place >= z, z > 0))
            def _():
                sent(owner, half, TO_PREV).wait_send()

        return carry

    lax.fori_loop(0, line, settle, 0)
    for group in range(groups):
        result(group).wait()


def local(count, queries, keys, values, span_ids):
    rows = queries.shape[0]
    head_dim = keys.shape[2]
    width = queries.shape[2]
    groups = width // head_dim
    span = rows // 2
    any_space = pl.BlockSpec(memory_space=pl.ANY)
    out = pl.pallas_call(
        functools.partial(kernel, count, head_dim),
        out_shape=jax.ShapeDtypeStruct((rows, width), jnp.bfloat16),
        in_specs=[pl.BlockSpec(memory_space=pltpu.SMEM), any_space, any_space, any_space],
        out_specs=any_space,
        scratch_shapes=[
            pltpu.VMEM((groups, rows, head_dim), jnp.bfloat16),
            pltpu.VMEM((count, 2, 2, span, head_dim), jnp.bfloat16),
            pltpu.VMEM((2, span, head_dim), jnp.bfloat16),
            pltpu.VMEM((2, groups, span, head_dim), jnp.float32),
            pltpu.VMEM((2, groups, span, head_dim), jnp.float32),
            pltpu.VMEM((2, groups, span, head_dim), jnp.float32),
            pltpu.VMEM((groups, rows, head_dim), jnp.bfloat16),
            pltpu.SemaphoreType.DMA((2 + groups, 2)),
            pltpu.SemaphoreType.DMA((groups,)),
            pltpu.SemaphoreType.DMA((count, 2, 3)),
            pltpu.SemaphoreType.DMA((count, 2)),
        ],
        compiler_params=pltpu.CompilerParams(
            collective_id=0, has_side_effects=True, vmem_limit_bytes=56 * 2**20
        ),
    )(
        span_ids,
        queries.reshape(rows, width),
        keys.reshape(rows, head_dim),
        values.reshape(rows, head_dim),
    )
    return out.reshape(rows, 1, width)


def solution(mesh):
    in_specs = (P("ctx", "head", None), P("ctx", "head", None), P("ctx", "head", None), P())
    out_specs = P("ctx", "head", None)
    body = functools.partial(local, mesh.shape["ctx"])
    return jax.shard_map(body, mesh=mesh, in_specs=in_specs, out_specs=out_specs, check_vma=False)
```

time: 214 us -> 68.2 us (0.32)
  Pallas kernels: 0 us -> 65.3 us
  matrix products: 47 us -> 0 us
  other arithmetic: 46.7 us -> 0 us
  loops' own time: 41.1 us -> 0 us
  local copies, waits for them, and re-layouts: 42.7 us -> 2.67 us
  waiting for transfers between devices: 27.4 us -> 0 us
  starting transfers between devices: 8.12 us -> 0 us
    pallas_call x0 -> x1, Pallas kernels: none -> 65.3 us  [local(): pl.pallas_call(functools.partial(kernel, count, head_dim), out_shape=jax....]
    dot_general x34 -> x0, matrix products: 47 us -> none  [the longest x17 32 us: update(): jnp.einsum('qgk,kd->qgd', weights.astype(jnp.bfloat16), value_block, pref...]
    another operation x36 -> x0, loops' own time: 41.1 us -> none  [the longest x4 39.4 us: absorb(): lax.scan(step, state, (key_buf.reshape(pieces, span_rows, head_dim), valu...]
    ppermute x6 -> x0, waiting for transfers between devices: 27.4 us -> none  [swapped(): return lax.ppermute(block, axis, route)]
    reduce_sum x34 -> x0, other arithmetic: 21.5 us -> none  [the longest x17 19.3 us: update(): weight_sum = weight_sum * factor + jnp.sum(weights, axis=2)]
    squeeze x16 -> x0, local copies, waits for them, and re-layouts: 17.7 us -> none  [absorb(): lax.scan(step, state, (key_buf.reshape(pieces, span_rows, head_dim), valu...]
    cond x87 -> x0, local copies, waits for them, and re-layouts: 17.2 us -> none
    reduce_min x16 -> x0, other arithmetic: 10.5 us -> none  [step(): jnp.min(key_pos) <= jnp.max(part_pos)]
  transfers between devices with their start and end apart: 6 -> 0, of which waited for: 2 -> 0; matrix products, arithmetic and copies ran while one was open for 31% -> 0% of each run, Pallas kernels for 0% -> 0%
where the time goes in v1:
time: 68.2 us; the launch traced here: 68 us
  Pallas kernels  65.3 us (96%)
  local copies, waits for them, and re-layouts  2.67 us (4%)
    pallas_call x1, Pallas kernels, local(): pl.pallas_call(functools.partial(kernel, count, head_dim), out_shape=jax....  65.3 us
    unnamed x1, local copies, waits for them, and re-layouts  2.67 us

profile of v1, /device:TPU:0, one launch (start us, length us, event | category | flops | bytes accessed | tf_op | source)
XLA Modules:
  0.0 68.0 jit_solution(16742856605876630851)
XLA Ops:
  0.0 65.3 %shard_map.46 = bf16[768,1024]{1,0:T(8,128)(2,1)} custom-call(s32[16]{0:T(128)} %ids.1, bf16[768,1024]{1,0:T(8,128)(2,1)} %bitcast.5, bf16[768,128]{1,0:T(8,128)(2,1)} %bitcast.6, bf16[768,128]{1,0:T(8,128)(2,1)} %bitcast.7), custom_call_target="tpu_custom_call" | custom-call | tf_op jit(solution)/shard_map/pallas_call | solution.py:283
  65.4 2.7 %copy.6 = bf16[768,1,1024]{2,0,1:T(8,128)(2,1)} copy(bf16[768,1,1024]{2,0,1:T(8,128)(2,1)} %bitcast.4) | data formatting | bytes 3145728

commit v2 on v1

--- a/solution.py
+++ b/solution.py
@@ -12,7 +12,8 @@
 LOW, HIGH = 0, 1
 TO_PARTNER, TO_NEXT, TO_PREV = 0, 1, 2
 MASKED = -1e30
-HEADS_PER_STEP = 2
+SLAB = 4
+SLABS_PER_STEP = 1
 
 
 def kernel(
@@ -23,7 +24,9 @@
     span = rows // 2
     line = count // 2
     lanes = head_dim
-    pieces = span // lanes
+    slab = math.gcd(groups, SLAB)
+    per_step = math.gcd(groups // slab, SLABS_PER_STEP)
+    tall = slab * span
     scale = head_dim ** (-0.5) * math.log2(math.e)
     me = lax.axis_index("ctx")
     z = me // 2
@@ -121,14 +124,14 @@
 
     def row_top(s):
         best = s[:, :lanes]
-        for piece in range(1, pieces):
+        for piece in range(1, s.shape[1] // lanes):
             best = jnp.maximum(best, s[:, piece * lanes : (piece + 1) * lanes])
         return jnp.max(best, axis=1, keepdims=True)
 
     def weigh(s, m):
         parts = [
             jnp.exp2((s[:, piece * lanes : (piece + 1) * lanes] - m) * scale)
-            for piece in range(pieces)
+            for piece in range(s.shape[1] // lanes)
         ]
         summed = parts[0]
         for part in parts[1:]:
@@ -140,70 +143,89 @@
 
     def over_groups(body):
         def step(index, carry):
-            for inner in range(HEADS_PER_STEP):
-                body(index * HEADS_PER_STEP + inner)
+            for inner in range(per_step):
+                body(pl.ds((index * per_step + inner) * slab, slab))
             return carry
 
-        lax.fori_loop(0, groups // HEADS_PER_STEP, step, 0)
+        lax.fori_loop(0, groups // (slab * per_step), step, 0)
 
     def half_q(group, half):
-        return q[group, half * span : (half + 1) * span, :]
+        return q[group, half * span : (half + 1) * span, :].reshape(tall, lanes)
+
+    def read(ref, half, group):
+        return ref[half, group].reshape(tall, lanes)
+
+    def write(ref, half, group, value):
+        ref[half, group] = value.reshape(slab, span, lanes)
 
     def own_span(half):
-        row_no = lax.broadcasted_iota(jnp.int32, (span, span), 0)
-        key_no = lax.broadcasted_iota(jnp.int32, (span, span), 1)
+        row_no = lax.broadcasted_iota(jnp.int32, (tall, span), 0) % span
+        key_no = lax.broadcasted_iota(jnp.int32, (tall, span), 1)
 
         def body(group):
             s = score(half_q(group, half), kv[me, half, 0])
             s = jnp.where(key_no <= row_no, s, MASKED)
-            m = jnp.broadcast_to(row_top(s), (span, lanes))
+            m = jnp.broadcast_to(row_top(s), (tall, lanes))
             p, summed = weigh(s, m)
-            top[half, group] = m
-            total[half, group] = summed
-            acc[half, group] = mix(p, kv[me, half, 1])
+            write(top, half, group, m)
+            write(total, half, group, summed)
+            write(acc, half, group, mix(p, kv[me, half, 1]))
 
         over_groups(body)
 
-    def high_on_low(owner):
+    def high_on_low(owners):
         def body(group):
-            s = score(half_q(group, HIGH), kv[owner, LOW, 0])
-            old = top[HIGH, group]
+            keys = jnp.concatenate([kv[owner, LOW, 0] for owner in owners], axis=0)
+            values = jnp.concatenate([kv[owner, LOW, 1] for owner in owners], axis=0)
+            s = score(half_q(group, HIGH), keys)
+            old = read(top, HIGH, group)
             m = jnp.maximum(old, row_top(s))
             fade = jnp.exp2((old - m) * scale)
             p, summed = weigh(s, m)
-            top[HIGH, group] = m
-            total[HIGH, group] = total[HIGH, group] * fade + summed
-            acc[HIGH, group] = acc[HIGH, group] * fade + mix(p, kv[owner, LOW, 1])
+            write(top, HIGH, group, m)
+            write(total, HIGH, group, read(total, HIGH, group) * fade + summed)
+            write(acc, HIGH, group, read(acc, HIGH, group) * fade + mix(p, values))
 
         over_groups(body)
 
-    def same_half(owner):
+    def one_same_half(owner):
         flag = jnp.where(ids[2 * owner] > ids[2 * me], 1, 0)
-        is_high = jnp.full((span, lanes), flag, jnp.int32) == 1
+        is_high = jnp.full((tall, lanes), flag, jnp.int32) == 1
+        key_high = jnp.full((span, lanes), flag, jnp.int32) == 1
         for which in range(2):
-            kv_pick[which] = jnp.where(is_high, kv[owner, HIGH, which], kv[owner, LOW, which])
+            kv_pick[which] = jnp.where(key_high, kv[owner, HIGH, which], kv[owner, LOW, which])
 
         def body(group):
             s = score(jnp.where(is_high, half_q(group, HIGH), half_q(group, LOW)), kv_pick[0])
-            tops = [top[half, group] for half in range(2)]
+            tops = [read(top, half, group) for half in range(2)]
             old = jnp.where(is_high, tops[HIGH], tops[LOW])
             m = jnp.maximum(old, row_top(s))
             fade = jnp.exp2((old - m) * scale)
             p, summed = weigh(s, m)
-            top[LOW, group] = jnp.where(is_high, tops[LOW], m)
-            top[HIGH, group] = jnp.where(is_high, m, tops[HIGH])
+            write(top, LOW, group, jnp.where(is_high, tops[LOW], m))
+            write(top, HIGH, group, jnp.where(is_high, m, tops[HIGH]))
             added = mix(p, kv_pick[1])
             for ref, extra in ((total, summed), (acc, added)):
-                low_now, high_now = ref[LOW, group], ref[HIGH, group]
+                low_now, high_now = read(ref, LOW, group), read(ref, HIGH, group)
                 new = jnp.where(is_high, high_now, low_now) * fade + extra
-                ref[LOW, group] = jnp.where(is_high, low_now, new)
-                ref[HIGH, group] = jnp.where(is_high, new, high_now)
+                write(ref, LOW, group, jnp.where(is_high, low_now, new))
+                write(ref, HIGH, group, jnp.where(is_high, new, high_now))
 
         over_groups(body)
+
+    def same_half(owners):
+        def one(index, carry):
+            owner = owners[0]
+            for place in range(1, len(owners)):
+                owner = jnp.where(index == place, owners[place], owner)
+            one_same_half(owner)
+            return carry
+
+        lax.fori_loop(0, len(owners), one, 0)
 
     own_span(LOW)
     own_span(HIGH)
-    high_on_low(me)
+    high_on_low((me,))
 
     short = jnp.minimum(z, line - 1 - z)
     far_side = jnp.where(z <= line - 1 - z, 1, -1)
@@ -213,29 +235,29 @@
         alone = far_side * (order - short)
         return z + jnp.where(order <= 2 * short, paired, alone)
 
+    def arrived(owner, half):
+        sent(owner, half, TO_PARTNER).wait_recv()
+
+    def crossed(order):
+        return jnp.where(order == 0, z, line_place(order)) * 2 + 1 - x
+
     def visit(index, carry):
-        on_line = index % 2
-        step = index // 2 + 1
-        order = index // 2 + on_line
-        owner = line_place(order) * 2 + jnp.where(on_line == 1, x, 1 - x)
-        moving = jnp.logical_and(on_line == 0, step < line)
-        for half in range(2):
-
-            @pl.when(moving)
-            def _():
-                relay(step, half)
-
-            @pl.when(on_line == 0)
-            def _():
-                sent(owner, half, TO_PARTNER).wait_recv()
-
-            if half == LOW:
-                high_on_low(owner)
-            else:
-                same_half(owner)
+        across = crossed(index)
+        along = line_place(index + 1) * 2 + x
+        relay(index + 1, LOW)
+        arrived(across, LOW)
+        high_on_low((across, along))
+        relay(index + 1, HIGH)
+        arrived(across, HIGH)
+        same_half((across, along))
         return carry
 
-    lax.fori_loop(0, count - 1, visit, 0)
+    lax.fori_loop(0, line - 1, visit, 0)
+    last = crossed(jnp.int32(line - 1))
+    arrived(last, LOW)
+    high_on_low((last,))
+    arrived(last, HIGH)
+    same_half((last,))
 
     def finish(group):
         for half in range(2):

time: 68.2 us -> 49.7 us (0.73)
  the two profiles are of different devices: /device:TPU:0 before, /device:TPU:16 now
where the time goes in v2:
time: 49.7 us; the launch traced here: 49.6 us
  Pallas kernels  46.9 us (94%)
  local copies, waits for them, and re-layouts  2.67 us (5%)
    pallas_call x1, Pallas kernels, local(): pl.pallas_call(functools.partial(kernel, count, head_dim), out_shape=jax....  46.9 us
    unnamed x1, local copies, waits for them, and re-layouts  2.67 us

profile of v2, /device:TPU:16, one launch (start us, length us, event | category | flops | bytes accessed | tf_op | source)
XLA Modules:
  0.0 49.6 jit_solution(14757075211580756192)
XLA Ops:
  0.0 46.9 %shard_map.46 = bf16[768,1024]{1,0:T(8,128)(2,1)} custom-call(s32[16]{0:T(128)} %ids.1, bf16[768,1024]{1,0:T(8,128)(2,1)} %bitcast.5, bf16[768,128]{1,0:T(8,128)(2,1)} %bitcast.6, bf16[768,128]{1,0:T(8,128)(2,1)} %bitcast.7), custom_call_target="tpu_custom_call" | custom-call | tf_op jit(solution)/shard_map/pallas_call | solution.py:305
  46.9 2.7 %copy.6 = bf16[768,1,1024]{2,0,1:T(8,128)(2,1)} copy(bf16[768,1,1024]{2,0,1:T(8,128)(2,1)} %bitcast.4) | data formatting | bytes 3145728
